TPU v7x, 32 devices: a whole 2x2x4 slice. The times are simulated.
32 devices in a mesh: dp: 8 (over z, x), pipe: 2 (over core), tensor: 2 (over y).
Axes of the slice: x: 2, y: 2, z: 4, core: 2. Of those that a mesh axis runs over, the one named last changes fastest.
Arguments:
- hidden: bfloat16 [2, 1024, 3584], P('pipe', 'dp', 'tensor'), may hold values from -6 to 6
- frozen_weight: bfloat16 [3584, 3584], P('dp', 'tensor'), may hold values from -1 to 1
- final_norm_gain: float32 [3584], P('tensor'), may hold values from 0.1 to 1.9
- adapter_down_maps: bfloat16 [8, 32, 3584], P(None, None, 'tensor'), may hold values from -0.09375 to 0.09375
- adapter_up_maps: bfloat16 [8, 32, 3584], P(None, None, 'tensor'), may hold values from -1 to 1
- tenant: int32 [2, 64], P('pipe'), may hold values from 0 to 7, as said below
- adapter: int32 [2], P('pipe'), may hold values from 0 to 7
Outputs:
- upstream_grad: bfloat16 [2, 1024, 3584], P('pipe', 'dp', 'tensor')
- grad_up: float32 [2, 32, 3584], P('pipe', None, 'tensor')
- grad_down: float32 [2, 32, 3584], P('pipe', None, 'tensor')
- row_loss: float32 [2, 64], P('pipe', 'dp')
Inputs may be any that keep to these rules, and one draw needn't show every extreme that they name: Rows 2i and 2i + 1 of a micro-batch have the same tenant.
All inputs are finite; a program needn't handle non-finite values.
Results may differ from a plain program's by a relative error of at most 0.024.
Values may be sent and summed in bfloat16 or wider, within the bound.
No kernel may reach another device: no remote copies, remote signals or barrier semaphores. Data moves between devices by JAX's collectives and lax.ppermute only.
A program may use at most 64 MiB of HBM per device.

v0:
```python
import jax
import jax.numpy as jnp
from jax import lax
from jax.sharding import PartitionSpec as P

MODEL_WIDTH = 3584
SEQ = 16
logit_divisor = 0.05
loss_scale = 256.0
adapter_scale = 0.5
epsilon = 1e-06


def passed_along(block, axis, distance):
    devices = range(lax.axis_size(axis))
    route = [((i - distance) % len(devices), i) for i in devices]
    return lax.ppermute(block, axis, route)


def body(
    hidden, frozen_weight, final_norm_gain, adapter_down_maps, adapter_up_maps, tenant, adapter
):
    own_tokens = hidden[0]
    token_count = own_tokens.shape[0]
    half_width = own_tokens.shape[1]
    rows_local = token_count // SEQ
    full_tokens = lax.all_gather(own_tokens, "tensor", axis=1, tiled=True)
    picked_adapter = adapter[0]
    down_matrix = lax.dynamic_index_in_dim(adapter_down_maps, picked_adapter, 0, keepdims=False)
    up_matrix = lax.dynamic_index_in_dim(adapter_up_maps, picked_adapter, 0, keepdims=False)
    low_part = lax.dot_general(
        own_tokens, down_matrix, (((1,), (1,)), ((), ())), preferred_element_type=jnp.float32
    )
    full_weight = lax.all_gather(frozen_weight, "dp", axis=0, tiled=True)
    frozen_output = jnp.dot(full_tokens, full_weight, preferred_element_type=jnp.float32)
    low_rank_hidden = lax.psum(low_part, "tensor").astype(jnp.bfloat16)
    output_rows = frozen_output + adapter_scale * jnp.dot(
        low_rank_hidden, up_matrix, preferred_element_type=jnp.float32
    )
    token_squares = lax.psum(jnp.sum(output_rows * output_rows, axis=1), "tensor")
    token_inv = lax.rsqrt(token_squares / MODEL_WIDTH + epsilon)
    gained = output_rows * final_norm_gain[None, :]
    normed = gained * token_inv[:, None]
    pooled = jnp.mean(normed.reshape(rows_local, SEQ, half_width), axis=1)
    squares = lax.psum(jnp.sum(pooled * pooled, axis=1), "tensor")
    inverse = lax.rsqrt(squares + epsilon)
    unit_rows = pooled * inverse[:, None]
    encoded_vectors = unit_rows.astype(jnp.bfloat16)
    all_rows = lax.all_gather(encoded_vectors, "dp", axis=0, tiled=True)
    total_rows = all_rows.shape[0]
    logit_blocks = lax.dot_general(
        encoded_vectors, all_rows, (((1,), (1,)), ((), ())), preferred_element_type=jnp.float32
    )
    cosine_logits = lax.psum(logit_blocks, "tensor") / logit_divisor
    position = lax.axis_index("dp")
    own_ids = position * rows_local + jnp.arange(rows_local, dtype=jnp.int32)
    every_id = jnp.arange(total_rows, dtype=jnp.int32)
    tenants_all = tenant[0]
    own_tenants = lax.dynamic_slice_in_dim(tenants_all, position * rows_local, rows_local)
    allowed = (own_tenants[:, None] == tenants_all[None, :]) & (
        own_ids[:, None] != every_id[None, :]
    )
    partner = every_id[None, :] == (own_ids ^ 1)[:, None]
    partner_float = partner.astype(jnp.float32)
    exps = jnp.where(allowed, jnp.exp(cosine_logits), 0.0)
    log_total = jnp.log(jnp.sum(exps, axis=1))
    positive = jnp.sum(jnp.where(partner, cosine_logits, 0.0), axis=1)
    row_loss = log_total - positive
    probs = jnp.where(allowed, jnp.exp(cosine_logits - log_total[:, None]), 0.0)
    weights = (loss_scale * (probs - partner_float)).astype(jnp.bfloat16)
    matching_logits = jnp.dot(weights, all_rows, preferred_element_type=jnp.float32)
    all_totals = lax.all_gather(log_total, "dp", axis=0, tiled=True)
    column_probs = jnp.where(allowed, jnp.exp(cosine_logits - all_totals[None, :]), 0.0)
    column_weights = (loss_scale * (column_probs - partner_float)).astype(jnp.bfloat16)
    groups = lax.axis_size("dp")
    grouped_weights = column_weights.reshape(rows_local, groups, rows_local)
    grouped_rows = all_rows.reshape(groups, rows_local, half_width)
    far_terms = jnp.einsum(
        "jki,kid->kjd", grouped_weights, grouped_rows, preferred_element_type=jnp.float32
    ).astype(jnp.bfloat16)
    far_terms = lax.optimization_barrier(far_terms)
    distractor_logits = jnp.sum(far_terms.astype(jnp.float32), axis=0)
    encoded_vector_derivative = (matching_logits + distractor_logits) / logit_divisor
    gained_rows = gained.reshape(rows_local, SEQ, half_width)
    along_part = jnp.sum(unit_rows * encoded_vector_derivative, axis=1)
    first_part = jnp.einsum("rsd,rd->rs", gained_rows, encoded_vector_derivative)
    second_part = jnp.einsum("rsd,rd->rs", gained_rows, unit_rows)
    along, first_sum, second_sum = lax.psum((along_part, first_part, second_part), "tensor")
    grad_pool = inverse[:, None] * (encoded_vector_derivative - unit_rows * along[:, None])
    inner = (inverse[:, None] * (first_sum - along[:, None] * second_sum) / SEQ).reshape(
        token_count
    )
    spread = jnp.broadcast_to(
        (grad_pool * final_norm_gain[None, :])[:, None, :] / SEQ, (rows_local, SEQ, half_width)
    ).reshape(token_count, half_width)
    grad_norm_in = token_inv[:, None] * (
        spread - output_rows * (inner * token_inv * token_inv / MODEL_WIDTH)[:, None]
    )
    output_gradient = grad_norm_in.astype(jnp.bfloat16)
    low_rank_grad_piece = adapter_scale * lax.dot_general(
        output_gradient, up_matrix, (((1,), (1,)), ((), ())), preferred_element_type=jnp.float32
    )
    low_rank_gradient = lax.psum(low_rank_grad_piece, "tensor").astype(jnp.bfloat16)
    base_terms = lax.dot_general(
        output_gradient, full_weight, (((1,), (1,)), ((), ())), preferred_element_type=jnp.float32
    )
    base_sum = lax.psum_scatter(
        base_terms.astype(jnp.bfloat16), "tensor", scatter_dimension=1, tiled=True
    ).astype(jnp.float32)
    grad_in = (
        base_sum + jnp.dot(low_rank_gradient, down_matrix, preferred_element_type=jnp.float32)
    ).astype(jnp.bfloat16)
    handed = passed_along(grad_in, "pipe", -1)
    up_map_piece = adapter_scale * lax.dot_general(
        low_rank_hidden,
        output_gradient,
        (((0,), (0,)), ((), ())),
        preferred_element_type=jnp.float32,
    )
    downward_part = lax.dot_general(
        low_rank_gradient, own_tokens, (((0,), (0,)), ((), ())), preferred_element_type=jnp.float32
    )
    up_map_gradient, grad_downward = (
        lax.psum(up_map_piece.astype(jnp.bfloat16), "dp").astype(jnp.float32),
        lax.psum(downward_part.astype(jnp.bfloat16), "dp").astype(jnp.float32),
    )
    return (handed[None], up_map_gradient[None], grad_downward[None], row_loss[None])


def solution(mesh):
    return jax.shard_map(
        body,
        mesh=mesh,
        in_specs=(
            P("pipe", "dp", "tensor"),
            P("dp", "tensor"),
            P("tensor"),
            P(None, None, "tensor"),
            P(None, None, "tensor"),
            P("pipe", None),
            P("pipe"),
        ),
        out_specs=(
            P("pipe", "dp", "tensor"),
            P("pipe", None, "tensor"),
            P("pipe", None, "tensor"),
            P("pipe", "dp"),
        ),
        check_vma=False,
    )
```

profile of v0, /device:TPU:0, one launch (start us, length us, event | category | flops | bytes accessed | tf_op | source)
XLA Modules:
  0.0 384.0 jit_solution(8150404245731243442)
XLA Ops:
  7.2 0.0 copy-start
  7.2 0.0 all-gather.3.cloned.1.call-start
  7.2 0.7 all-gather.3.cloned.1.call-update
  7.9 0.0 copy-start.2
  7.9 0.0 reduce-scatter.2.cloned.1.call-start
  8.6 1.2 dynamic-slice.1
  9.9 1.3 convolution_bitcast_fusion
  11.2 9.8 %psum.70 = bf16[128,32]{0,1:T(8,128)(2,1)S(1)} all-reduce(f32[128,32]{0,1:T(8,128)S(1)} %convolution_bitcast_fusion), channel_id=1, replica_groups=mesh['dp'=8,'pipe'=2,'tensor'=2] {'tensor'}, use_global_device_ids=true, to_apply=%region_0.1 | all-reduce | flops 4096 | bytes 24576 | tf_op jit(solution)/shard_map/psum | solution.py:36
  20.9 0.7 fusion.48
  21.7 11.0 %all-gather = bf16[1,128,3584]{2,1,0:T(8,128)(2,1)S(1)} all-gather(bf16[1,128,1792]{2,1,0:T(8,128)(2,1)} %param.7), channel_id=2, replica_groups=mesh['dp'=8,'pipe'=2,'tensor'=2] {'tensor'}, dimensions={2}, use_global_device_ids=true | all-gather | bytes 1376256 | tf_op jit(solution)/shard_map/all_gather | solution.py:27
  32.7 0.0 copy-start.3
  32.7 159.5 %all-gather.3.cloned.1.call-done = bf16[3584,1792]{1,0:T(8,128)(2,1)} async-done(((bf16[448,1792]{1,0:T(8,128)(2,1)}), bf16[3584,1792]{1,0:T(8,128)(2,1)}) %all-gather.3.cloned.1.call-update) | async-done | bytes 12845072 | tf_op jit(solution)/shard_map/all_gather | solution.py:34
  192.2 6.5 %fusion.8 = f32[128,1792]{1,0:T(8,128)S(1)} fusion(bf16[3584,1792]{1,0:T(8,128)(2,1)} %all-gather.3.cloned.1.call-done, bf16[1,128,3584]{2,1,0:T(8,128)(2,1)S(1)} %all-gather), kind=kOutput, calls=%fused_computation.19 | convolution fusion | flops 1644167168 | bytes 14680064 | tf_op jit(solution)/shard_map/dot_general | solution.py:35
  198.7 0.0 copy-done
  198.7 0.0 copy-start.1
  198.7 0.4 multiply_reduce_fusion
  199.1 4.9 %psum.71 = f32[128]{0:T(128)S(1)} all-reduce(f32[128]{0:T(128)S(1)} %get-tuple-element.18), channel_id=1, replica_groups=mesh['dp'=8,'pipe'=2,'tensor'=2] {'tensor'}, use_global_device_ids=true, to_apply=%region_2.3 | all-reduce | flops 128 | bytes 1024 | tf_op jit(solution)/shard_map/psum | solution.py:40
  204.1 0.0 copy-done.2
  204.1 0.3 bitcast_reduce_fusion
  204.3 0.1 multiply_reduce_fusion.2
  205.1 4.9 %psum.72 = f32[8]{0:T(128)S(1)} all-reduce(f32[8]{0:T(128)S(1)} %multiply_reduce_fusion.2), channel_id=1, replica_groups=mesh['dp'=8,'pipe'=2,'tensor'=2] {'tensor'}, use_global_device_ids=true, to_apply=%region_5.6 | all-reduce | flops 8 | bytes 64 | tf_op jit(solution)/shard_map/psum | solution.py:45
  210.1 0.1 multiply_convert_fusion
  210.1 0.1 multiply_bitcast_fusion
  210.2 30.7 %all_gather.14 = bf16[64,1792]{1,0:T(8,128)(2,1)S(1)} all-gather(bf16[8,1792]{1,0:T(8,128)(2,1)S(1)} %multiply_convert_fusion), channel_id=1, replica_groups=mesh['dp'=8,'pipe'=2,'tensor'=2] {'dp'}, dimensions={0}, use_global_device_ids=true | all-gather | bytes 258048 | tf_op jit(solution)/shard_map/all_gather | solution.py:49
  240.9 0.1 fusion.53
  241.1 5.0 %psum.73 = f32[8,64]{1,0:T(8,128)S(1)} all-reduce(f32[8,64]{1,0:T(8,128)S(1)} %fusion.53), channel_id=1, replica_groups=mesh['dp'=8,'pipe'=2,'tensor'=2] {'tensor'}, use_global_device_ids=true, to_apply=%region_6.7 | all-reduce | flops 512 | bytes 4096 | tf_op jit(solution)/shard_map/psum | solution.py:54
  246.0 0.0 copy-done.3
  246.0 0.2 select_reduce_fusion
  246.2 0.5 subtract_bitcast_fusion
  246.8 18.5 %all-reduce = f32[64]{0:T(128)S(1)} all-reduce(f32[64]{0:T(128)S(1)} %get-tuple-element.14), channel_id=1, replica_groups=mesh['dp'=8,'pipe'=2,'tensor'=2] {'dp'}, use_global_device_ids=true, to_apply=%add | all-reduce | flops 64 | bytes 512
  265.3 0.1 fusion.29
  265.4 0.1 reshape.64
  265.4 0.2 convolution_convert_fusion.1
  265.7 0.3 multiply_reduce_fusion.1
  266.0 0.2 fusion.23
  266.2 0.2 fusion.21
  266.5 5.0 %all-reduce.1 = (f32[8,16]{1,0:T(8,128)S(1)}, f32[8,16]{1,0:T(8,128)S(1)}, f32[8]{0:T(128)S(1)}) all-reduce(f32[8,16]{1,0:T(8,128)S(1)} %bitcast.74, f32[8,16]{1,0:T(8,128)S(1)} %bitcast.75, f32[8]{0:T(128)S(1)} %get-tuple-element.20), channel_id=1, replica_groups=mesh['dp'=8,'pipe'=2,'tensor'=2] {'tensor'}, use_global_device_ids=true, to_apply=%region_11.12 | all-reduce | flops 264 | bytes 2112 | tf_op jit(solution)/shard_map/psum | solution.py:88
  271.5 0.1 multiply_multiply_fusion
  271.6 0.1 multiply_multiply_fusion.1
  271.7 0.1 reshape.68
  271.8 0.2 fusion.7
  272.0 9.9 %convolution_convert_fusion = bf16[128,3584]{1,0:T(8,128)(2,1)} fusion(bf16[128,1792]{1,0:T(8,128)(2,1)S(1)} %fusion.7, bf16[3584,1792]{1,0:T(8,128)(2,1)} %all-gather.3.cloned.1.call-done), kind=kOutput, calls=%fused_computation | convolution fusion | flops 1644625920 | bytes 14221312 | tf_op jit(solution)/shard_map/dot_general | solution.py:104
  281.9 0.0 reduce-scatter.2.cloned.1.call-update
  281.9 0.0 all-reduce.5.cloned.1.call-start
  282.0 0.2 convolution_multiply_fusion.2
  282.2 8.5 %psum.77 = bf16[128,32]{0,1:T(8,128)(2,1)S(1)} all-reduce(f32[128,32]{0,1:T(8,128)S(1)} %convolution_multiply_fusion.2), channel_id=1, replica_groups=mesh['dp'=8,'pipe'=2,'tensor'=2] {'tensor'}, use_global_device_ids=true, to_apply=%region_14.15 | all-reduce | flops 4096 | bytes 24576 | tf_op jit(solution)/shard_map/psum | solution.py:103
  290.7 7.7 %reduce-scatter.2.cloned.1.call-done = bf16[128,1792]{1,0:T(8,128)(2,1)} async-done(((bf16[128,3584]{1,0:T(8,128)(2,1)}), bf16[128,1792]{1,0:T(8,128)(2,1)}) %reduce-scatter.2.cloned.1.call-update) | async-done | bytes 458768 | tf_op jit(solution)/shard_map/reduce_scatter | solution.py:107
  298.4 1.4 fusion.1
  299.8 0.1 collective-permute-start
  299.9 0.8 fusion.4
  300.8 0.0 copy-done.1
  300.8 0.8 fusion.3
  301.6 0.0 all-reduce.5.cloned.1.call-update
  301.6 71.9 %all-reduce.5.cloned.1.call-done = (bf16[1,32,1792]{2,1,0:T(8,128)(2,1)}, bf16[1,32,1792]{2,1,0:T(8,128)(2,1)}) async-done(((bf16[1,32,1792]{2,1,0:T(8,128)(2,1)}, bf16[1,32,1792]{2,1,0:T(8,128)(2,1)}), (bf16[1,32,1792]{2,1,0:T(8,128)(2,1)}, bf16[1,32,1792]{2,1,0:T(8,128)(2,1)})) %all-reduce.5.cloned.1.call-update) | async-done | bytes 229392 | tf_op jit(solution)/shard_map/psum | solution.py:124
  373.5 1.6 broadcast_in_dim.25
  375.1 1.6 broadcast_in_dim.52
  376.7 0.0 collective-permute-done
  376.7 0.8 copy.27
  (6 shorter events, 0.1 us)
Async XLA Ops:
  7.2 191.5 %copy-start = (bf16[8,32,1792]{2,1,0:T(8,128)(2,1)S(1)}, bf16[8,32,1792]{2,1,0:T(8,128)(2,1)}, u32[]{:S(2)}) copy-start(bf16[8,32,1792]{2,1,0:T(8,128)(2,1)} %param.11) | copy-start | bytes 2752516
  7.2 185.0 %all-gather.3.cloned.1.call-start = ((), (), s32[]{:S(2)}) async-start(), calls=%async_computation.1 | async-start | bytes 14450688 | tf_op jit(solution)/shard_map/all_gather | solution.py:34
  7.9 196.2 %copy-start.2 = (f32[1792]{0:T(1024)S(1)}, f32[1792]{0:T(1024)}, u32[]{:S(2)}) copy-start(f32[1792]{0:T(1024)} %param.9) | copy-start | bytes 21508
  7.9 290.5 %reduce-scatter.2.cloned.1.call-start = ((), (), s32[]{:S(2)}) async-start(), calls=%async_computation.2 | async-start | bytes 1376256 | tf_op jit(solution)/shard_map/reduce_scatter | solution.py:107
  32.7 213.3 %copy-start.3 = (s32[1,64]{1,0:T(1,128)S(1)}, s32[1,64]{1,0:T(1,128)}, u32[]{:S(2)}) copy-start(s32[1,64]{1,0:T(1,128)} %param.12) | copy-start | bytes 772
  198.7 102.0 %copy-start.1 = (bf16[1,128,1792]{2,1,0:T(8,128)(2,1)S(1)}, bf16[1,128,1792]{2,1,0:T(8,128)(2,1)}, u32[]{:S(2)}) copy-start(bf16[1,128,1792]{2,1,0:T(8,128)(2,1)} %param.7) | copy-start | bytes 1376260
  281.9 91.6 %all-reduce.5.cloned.1.call-start = ((), (), s32[]{:S(2)}) async-start(), calls=%async_computation.3 | async-start | bytes 458752 | tf_op jit(solution)/shard_map/psum | solution.py:124
  299.8 76.9 %collective-permute-start = (bf16[128,1792]{1,0:T(8,128)(2,1)S(1)}, bf16[128,1792]{1,0:T(8,128)(2,1)S(1)}, u32[]{:S(2)}, u32[]{:S(2)}) collective-permute-start(bf16[128,1792]{1,0:T(8,128)(2,1)S(1)} %fusion.1), channel_id=1, source_target_pairs={{2,0},{0,2},{3,1},{1,3},{6,4},{4,6},{7,5},{5,7},{10,8},{8,10},{11,... | collective-permute-start | bytes 1376264 | tf_op jit(solution)/shard_map/ppermute | solution.py:17
Sparse Core Ops, SparseCore 0:
  10.2 182.0 all-gather.2
  282.0 16.3 reduce-scatter.1
  302.5 70.9 all-reduce.4
where the time goes:
time: 385 us; the launch traced here: 384 us
  waiting for transfers between devices  240 us (62%)
  blocking collectives  98.4 us (26%)
  matrix products  22.5 us (6%)
  between operations  15.2 us (4%)
  other arithmetic  4.98 us (1%)
    all_gather x1, waiting for transfers between devices, body(): full_weight = lax.all_gather(frozen_weight, 'dp', axis=0, tiled=True)  160 us
    psum x1, waiting for transfers between devices, body(): lax.psum(up_map_piece.astype(jnp.bfloat16), 'dp').astype(jnp.float32)  71.9 us
    all_gather x1, blocking collectives, body(): all_rows = lax.all_gather(encoded_vectors, 'dp', axis=0, tiled=True)  30.7 us
    unnamed x1, blocking collectives  18.5 us
    all_gather x1, blocking collectives, body(): full_tokens = lax.all_gather(own_tokens, 'tensor', axis=1, tiled=True)  11 us
    dot_general x1, matrix products, body(): lax.dot_general(output_gradient, full_weight, (((1,), (1,)), ((), ())), p...  9.88 us
    psum x1, blocking collectives, body(): low_rank_hidden = lax.psum(low_part, 'tensor').astype(jnp.bfloat16)  9.75 us
    psum x1, blocking collectives, body(): lax.psum(low_rank_grad_piece, 'tensor').astype(jnp.bfloat16)  8.55 us
  transfers between devices with their start and end apart: 4, of which 3 were waited for; matrix products, arithmetic and copies ran while one was open for 2% of the time, Pallas kernels for 0%

commit v1 on v0

--- a/solution.py
+++ b/solution.py
@@ -121,7 +121,9 @@
         low_rank_gradient, own_tokens, (((0,), (0,)), ((), ())), preferred_element_type=jnp.float32
     )
     up_map_gradient, grad_downward = (
-        lax.psum(up_map_piece.astype(jnp.bfloat16), "dp").astype(jnp.float32),
+        jnp.sum(lax.all_gather(up_map_piece.astype(jnp.bfloat16), "dp"), axis=0).astype(
+            jnp.float32
+        ),
         lax.psum(downward_part.astype(jnp.bfloat16), "dp").astype(jnp.float32),
     )
     return (handed[None], up_map_gradient[None], grad_downward[None], row_loss[None])

time: 385 us -> 402 us (1.044)
  blocking collectives: 98.4 us -> 131 us
  waiting for transfers between devices: 240 us -> 226 us
    all_gather x0 -> x1, blocking collectives: none -> 32.1 us  [body(): lax.all_gather(up_map_piece.astype(jnp.bfloat16), 'dp')]
    reduce_scatter x1, waiting for transfers between devices: 7.69 us -> 0.01 us  [body(): lax.psum_scatter(base_terms.astype(jnp.bfloat16), 'tensor', scatter_dimen...]
    psum x1, waiting for transfers between devices: 71.9 us -> 65.8 us  [body(): lax.psum(downward_part.astype(jnp.bfloat16), 'dp').astype(jnp.float32)]
  transfers between devices with their start and end apart: 4 -> 4, of which waited for: 3 -> 2; matrix products, arithmetic and copies ran while one was open for 2% -> 2% of each run, Pallas kernels for 0% -> 0%
where the time goes in v1:
time: 402 us
  waiting for transfers between devices  226 us (56%)
  blocking collectives  131 us (33%)
  matrix products  22.6 us (6%)
  between operations  15.2 us (4%)
  other arithmetic  4.21 us (1%)
    all_gather x1, waiting for transfers between devices, body(): full_weight = lax.all_gather(frozen_weight, 'dp', axis=0, tiled=True)  160 us
    psum x1, waiting for transfers between devices, body(): lax.psum(downward_part.astype(jnp.bfloat16), 'dp').astype(jnp.float32)  65.8 us
    all_gather x1, blocking collectives, body(): lax.all_gather(up_map_piece.astype(jnp.bfloat16), 'dp')  32.1 us
    all_gather x1, blocking collectives, body(): all_rows = lax.all_gather(encoded_vectors, 'dp', axis=0, tiled=True)  30.7 us
    unnamed x1, blocking collectives  18.5 us
    all_gather x1, blocking collectives, body(): full_tokens = lax.all_gather(own_tokens, 'tensor', axis=1, tiled=True)  11 us
    dot_general x1, matrix products, body(): lax.dot_general(output_gradient, full_weight, (((1,), (1,)), ((), ())), p...  9.88 us
    psum x1, blocking collectives, body(): low_rank_hidden = lax.psum(low_part, 'tensor').astype(jnp.bfloat16)  9.75 us
  transfers between devices with their start and end apart: 4, of which 2 were waited for; matrix products, arithmetic and copies ran while one was open for 2% of the time, Pallas kernels for 0%

profile of v1, /device:TPU:0, one launch (start us, length us, event | category | flops | bytes accessed | tf_op | source)
XLA Modules:
  0.0 401.8 jit_solution(18201863117315301059)
XLA Ops:
  7.2 0.0 copy-start
  7.2 0.0 all-gather.4.cloned.1.call-start
  7.2 0.7 all-gather.4.cloned.1.call-update
  7.9 0.0 copy-start.2
  7.9 0.0 reduce-scatter.2.cloned.1.call-start
  8.6 1.2 dynamic-slice.1
  9.9 1.3 convolution_bitcast_fusion
  11.2 9.8 %psum.63 = bf16[128,32]{0,1:T(8,128)(2,1)S(1)} all-reduce(f32[128,32]{0,1:T(8,128)S(1)} %convolution_bitcast_fusion), channel_id=1, replica_groups=mesh['dp'=8,'pipe'=2,'tensor'=2] {'tensor'}, use_global_device_ids=true, to_apply=%region_0.1 | all-reduce | flops 4096 | bytes 24576 | tf_op jit(solution)/shard_map/psum | solution.py:36
  20.9 0.7 fusion.47
  21.7 11.0 %all-gather = bf16[1,128,3584]{2,1,0:T(8,128)(2,1)S(1)} all-gather(bf16[1,128,1792]{2,1,0:T(8,128)(2,1)} %param.7), channel_id=2, replica_groups=mesh['dp'=8,'pipe'=2,'tensor'=2] {'tensor'}, dimensions={2}, use_global_device_ids=true | all-gather | bytes 1376256 | tf_op jit(solution)/shard_map/all_gather | solution.py:27
  32.7 0.0 copy-start.3
  32.7 159.5 %all-gather.4.cloned.1.call-done = bf16[3584,1792]{1,0:T(8,128)(2,1)} async-done(((bf16[448,1792]{1,0:T(8,128)(2,1)}), bf16[3584,1792]{1,0:T(8,128)(2,1)}) %all-gather.4.cloned.1.call-update) | async-done | bytes 12845072 | tf_op jit(solution)/shard_map/all_gather | solution.py:34
  192.2 6.5 %fusion.7 = f32[128,1792]{1,0:T(8,128)S(1)} fusion(bf16[3584,1792]{1,0:T(8,128)(2,1)} %all-gather.4.cloned.1.call-done, bf16[1,128,3584]{2,1,0:T(8,128)(2,1)S(1)} %all-gather), kind=kOutput, calls=%fused_computation.18 | convolution fusion | flops 1644167168 | bytes 14680064 | tf_op jit(solution)/shard_map/dot_general | solution.py:35
  198.7 0.0 copy-done
  198.7 0.4 multiply_reduce_fusion
  199.1 0.0 copy-start.1
  199.1 5.1 %psum.64 = f32[128]{0:T(128)S(1)} all-reduce(f32[128]{0:T(128)S(1)} %get-tuple-element.16), channel_id=1, replica_groups=mesh['dp'=8,'pipe'=2,'tensor'=2] {'tensor'}, use_global_device_ids=true, to_apply=%region_2.3 | all-reduce | flops 128 | bytes 1024 | tf_op jit(solution)/shard_map/psum | solution.py:40
  204.2 0.0 copy-done.2
  204.2 0.3 bitcast_reduce_fusion
  204.5 0.1 multiply_reduce_fusion.2
  205.3 4.9 %psum.65 = f32[8]{0:T(128)S(1)} all-reduce(f32[8]{0:T(128)S(1)} %multiply_reduce_fusion.2), channel_id=1, replica_groups=mesh['dp'=8,'pipe'=2,'tensor'=2] {'tensor'}, use_global_device_ids=true, to_apply=%region_5.6 | all-reduce | flops 8 | bytes 64 | tf_op jit(solution)/shard_map/psum | solution.py:45
  210.2 0.1 multiply_convert_fusion
  210.3 0.1 multiply_bitcast_fusion
  210.3 30.7 %all_gather.20 = bf16[64,1792]{1,0:T(8,128)(2,1)S(1)} all-gather(bf16[8,1792]{1,0:T(8,128)(2,1)S(1)} %multiply_convert_fusion), channel_id=1, replica_groups=mesh['dp'=8,'pipe'=2,'tensor'=2] {'dp'}, dimensions={0}, use_global_device_ids=true | all-gather | bytes 258048 | tf_op jit(solution)/shard_map/all_gather | solution.py:49
  241.0 0.1 fusion.52
  241.2 5.0 %psum.66 = f32[8,64]{1,0:T(8,128)S(1)} all-reduce(f32[8,64]{1,0:T(8,128)S(1)} %fusion.52), channel_id=1, replica_groups=mesh['dp'=8,'pipe'=2,'tensor'=2] {'tensor'}, use_global_device_ids=true, to_apply=%region_6.7 | all-reduce | flops 512 | bytes 4096 | tf_op jit(solution)/shard_map/psum | solution.py:54
  246.1 0.0 copy-done.3
  246.1 0.2 select_reduce_fusion
  246.3 0.5 subtract_bitcast_fusion
  246.9 18.5 %all-reduce = f32[64]{0:T(128)S(1)} all-reduce(f32[64]{0:T(128)S(1)} %get-tuple-element.12), channel_id=1, replica_groups=mesh['dp'=8,'pipe'=2,'tensor'=2] {'dp'}, use_global_device_ids=true, to_apply=%add | all-reduce | flops 64 | bytes 512
  265.4 0.1 fusion.28
  265.5 0.1 reshape.73
  265.6 0.2 convolution_convert_fusion.1
  265.8 0.3 multiply_reduce_fusion.1
  266.1 0.2 fusion.22
  266.4 0.2 fusion.20
  266.6 5.0 %all-reduce.1 = (f32[8,16]{1,0:T(8,128)S(1)}, f32[8,16]{1,0:T(8,128)S(1)}, f32[8]{0:T(128)S(1)}) all-reduce(f32[8,16]{1,0:T(8,128)S(1)} %bitcast.77, f32[8,16]{1,0:T(8,128)S(1)} %bitcast.78, f32[8]{0:T(128)S(1)} %get-tuple-element.18), channel_id=1, replica_groups=mesh['dp'=8,'pipe'=2,'tensor'=2] {'tensor'}, use_global_device_ids=true, to_apply=%region_11.12 | all-reduce | flops 264 | bytes 2112 | tf_op jit(solution)/shard_map/psum | solution.py:88
  271.6 0.1 multiply_multiply_fusion
  271.7 0.1 multiply_multiply_fusion.1
  271.8 0.1 reshape.77
  271.9 0.2 fusion.6
  272.1 9.9 %convolution_convert_fusion = bf16[128,3584]{1,0:T(8,128)(2,1)} fusion(bf16[128,1792]{1,0:T(8,128)(2,1)S(1)} %fusion.6, bf16[3584,1792]{1,0:T(8,128)(2,1)} %all-gather.4.cloned.1.call-done), kind=kOutput, calls=%fused_computation | convolution fusion | flops 1644625920 | bytes 14221312 | tf_op jit(solution)/shard_map/dot_general | solution.py:104
  282.0 0.0 reduce-scatter.2.cloned.1.call-update
  282.0 0.0 all-reduce.4.cloned.1.call-start
  282.1 0.2 convolution_multiply_fusion.2
  282.3 8.6 %psum.70 = bf16[128,32]{0,1:T(8,128)(2,1)S(1)} all-reduce(f32[128,32]{0,1:T(8,128)S(1)} %convolution_multiply_fusion.2), channel_id=1, replica_groups=mesh['dp'=8,'pipe'=2,'tensor'=2] {'tensor'}, use_global_device_ids=true, to_apply=%region_14.15 | all-reduce | flops 4096 | bytes 24576 | tf_op jit(solution)/shard_map/psum | solution.py:103
  290.9 0.2 fusion.2
  291.1 32.1 %all-gather.1 = bf16[256,1792]{1,0:T(8,128)(2,1)S(1)} all-gather(bf16[32,1792]{1,0:T(8,128)(2,1)S(1)} %fusion.2), channel_id=3, replica_groups=mesh['dp'=8,'pipe'=2,'tensor'=2] {'dp'}, dimensions={0}, use_global_device_ids=true | all-gather | bytes 1032192 | tf_op jit(solution)/shard_map/all_gather | solution.py:124
  323.2 0.0 reduce-scatter.2.cloned.1.call-done
  323.3 2.2 fusion.1
  325.4 0.0 collective-permute-start
  325.4 0.0 copy-done.1
  325.4 0.8 fusion.3
  326.3 0.0 all-reduce.4.cloned.1.call-update
  326.3 0.1 reduce_sum.81
  326.4 0.7 bitcast_convert_fusion
  327.1 65.8 %all-reduce.4.cloned.1.call-done = bf16[1,32,1792]{2,1,0:T(8,128)(2,1)} async-done(((bf16[1,32,1792]{2,1,0:T(8,128)(2,1)}), bf16[1,32,1792]{2,1,0:T(8,128)(2,1)}) %all-reduce.4.cloned.1.call-update) | async-done | bytes 114704 | tf_op jit(solution)/shard_map/psum | solution.py:127
  392.9 1.6 broadcast_in_dim.20
  394.5 0.0 collective-permute-done
  394.5 0.8 copy.26
  (6 shorter events, 0.1 us)
Async XLA Ops:
  7.2 191.5 %copy-start = (bf16[8,32,1792]{2,1,0:T(8,128)(2,1)S(1)}, bf16[8,32,1792]{2,1,0:T(8,128)(2,1)}, u32[]{:S(2)}) copy-start(bf16[8,32,1792]{2,1,0:T(8,128)(2,1)} %param.11) | copy-start | bytes 2752516
  7.2 185.0 %all-gather.4.cloned.1.call-start = ((), (), s32[]{:S(2)}) async-start(), calls=%async_computation.1 | async-start | bytes 14450688 | tf_op jit(solution)/shard_map/all_gather | solution.py:34
  7.9 196.3 %copy-start.2 = (f32[1792]{0:T(1024)S(1)}, f32[1792]{0:T(1024)}, u32[]{:S(2)}) copy-start(f32[1792]{0:T(1024)} %param.9) | copy-start | bytes 21508
  7.9 315.3 %reduce-scatter.2.cloned.1.call-start = ((), (), s32[]{:S(2)}) async-start(), calls=%async_computation.2 | async-start | bytes 1376256 | tf_op jit(solution)/shard_map/reduce_scatter | solution.py:107
  32.7 213.4 %copy-start.3 = (s32[1,64]{1,0:T(1,128)S(1)}, s32[1,64]{1,0:T(1,128)}, u32[]{:S(2)}) copy-start(s32[1,64]{1,0:T(1,128)} %param.12) | copy-start | bytes 772
  199.1 126.3 %copy-start.1 = (bf16[1,128,1792]{2,1,0:T(8,128)(2,1)S(1)}, bf16[1,128,1792]{2,1,0:T(8,128)(2,1)}, u32[]{:S(2)}) copy-start(bf16[1,128,1792]{2,1,0:T(8,128)(2,1)} %param.7) | copy-start | bytes 1376260
  282.0 110.9 %all-reduce.4.cloned.1.call-start = ((), (), s32[]{:S(2)}) async-start(), calls=%async_computation.3 | async-start | bytes 229376 | tf_op jit(solution)/shard_map/psum | solution.py:127
  325.4 69.1 %collective-permute-start = (bf16[128,1792]{1,0:T(8,128)(2,1)}, bf16[128,1792]{1,0:T(8,128)(2,1)S(1)}, u32[]{:S(2)}, u32[]{:S(2)}) collective-permute-start(bf16[128,1792]{1,0:T(8,128)(2,1)} %fusion.1), channel_id=1, source_target_pairs={{2,0},{0,2},{3,1},{1,3},{6,4},{4,6},{7,5},{5,7},{10,8},{8,10},{11,... | collective-permute-start | bytes 1376264 | tf_op jit(solution)/shard_map/ppermute | solution.py:17
Sparse Core Ops, SparseCore 0:
  10.2 182.0 all-gather.3
  282.2 16.3 reduce-scatter.1
  326.4 66.4 all-reduce.3
